TPU v7x, 32 devices: a whole 2x2x4 slice. The times are simulated.
32 devices in a mesh: context: 2 (over core), tensor: 4 (over y, x), fsdp: 4 (over z).
Axes of the slice: x: 2, y: 2, z: 4, core: 2. Of those that a mesh axis runs over, the one named last changes fastest.
Arguments:
- input_raw: bfloat16 [4, 1024, 5120], P('fsdp', ('context', 'tensor')), may hold values from -6 to 6
- state_proj_raw: bfloat16 [4, 1024, 256], P('fsdp', ('context', 'tensor')), may hold values from -6 to 6
- gate_branch: bfloat16 [4, 1024, 5120], P('fsdp', ('context', 'tensor')), may hold values from -6 to 6
- step_raw: bfloat16 [4, 1024, 80], P('fsdp', ('context', 'tensor')), may hold values from -6 to 6
- convolution_taps: float32 [4, 5376], replicated, may hold values from -3 to 3
- convolution_bias: float32 [5376], replicated, may hold values from -3 to 3
- step_bias: float32 [80], P('tensor'), may hold values from -1.5 to 0.5
- decay_log_rate: float32 [80], P('tensor'), may hold values from -13 to -2, as said below
- skip_weight: float32 [80], P('tensor'), may hold values from 0.5 to 2
- gated_norm_gain: float32 [5120], P('tensor'), may hold values from 0.1 to 1.9
- output_weight: bfloat16 [5120, 2560], P('tensor', 'fsdp'), may hold values from -0.078125 to 0.078125
- adapter_down: bfloat16 [5120, 16], P('tensor'), may hold values from -0.078125 to 0.078125
- adapter_up: bfloat16 [16, 2560], replicated, may hold values from -0.29882812 to 0.29882812
- cotangent: bfloat16 [4, 1024, 2560], P('fsdp', ('context', 'tensor')), may hold values from -6 to 6
Outputs:
- mixed: bfloat16 [4, 1024, 2560], P('fsdp', ('context', 'tensor'))
- grad_a: float32 [5120, 16], P('tensor')
- grad_b: float32 [16, 2560], replicated
Inputs may be any that keep to these rules, and one draw needn't show every extreme that they name: `decay_log_rate`: logarithms of positive decay rates.
All inputs are finite; a program needn't handle non-finite values.
Results may differ from a plain program's by a relative error of at most 0.017.
Values may be sent and summed in bfloat16 or wider, within the bound.
No kernel may reach another device: no remote copies, remote signals or barrier semaphores. Data moves between devices by JAX's collectives and lax.ppermute only.
A program may use at most 128 MiB of HBM per device.

v0:
```python
import math
import jax
import jax.numpy as jnp
from jax import lax
from jax.sharding import PartitionSpec as P

epsilon = 1e-05


def passed_along(value, axis, steps):
    count = lax.axis_size(axis)
    leading, last = (max(0, -steps), min(count, count - steps))
    return lax.ppermute(value, axis, [(source, source + steps) for source in range(leading, last)])


def entering(value, axis, join, neutral):
    count, mine = (lax.axis_size(axis), lax.axis_index(axis))
    pieces = jax.tree.map(lambda part: lax.all_gather(part, axis), value)
    subtotal = jax.tree.map(
        lambda part, zero: jnp.full_like(part, 0) + jnp.asarray(zero, part.dtype), value, neutral
    )

    def lap(position, subtotal):
        longer = join(subtotal, jax.tree.map(lambda part: part[position], pieces))
        return jax.tree.map(lambda new, old: jnp.where(position < mine, new, old), longer, subtotal)

    return lax.fori_loop(0, count - 1, lap, subtotal)


def convolve(values, before, weight, bias_row):
    length = values.shape[0]
    extended = jnp.concatenate([before, values], axis=0)
    pre_act = bias_row[None, :] + weight[0][None, :] * extended[0:length].astype(jnp.float32)
    for tap_index in range(1, weight.shape[0]):
        pre_act = pre_act + weight[tap_index][None, :] * extended[
            tap_index : tap_index + length
        ].astype(jnp.float32)
    return jax.nn.silu(pre_act).astype(jnp.bfloat16)


def ssd_blocks(x_heads, b_rows, c_rows, step_size, log_decay, block_len):
    highest = lax.Precision.HIGHEST
    length = x_heads.shape[0]
    head_count = x_heads.shape[1]
    head_size = x_heads.shape[2]
    state_size = b_rows.shape[1]
    blocks = length // block_len
    causal = jnp.arange(block_len)[:, None] >= jnp.arange(block_len)[None, :]

    def advance(state_now, pieces):
        x_block, b_block, c_block, step_block, decay_block = pieces
        cum_decay = jnp.cumsum(decay_block, axis=0)
        cum_heads = cum_decay.T
        gap_decay = cum_heads[:, :, None] - cum_heads[:, None, :]
        decay_mat = jnp.where(causal[None], jnp.exp(jnp.where(causal[None], gap_decay, 0.0)), 0.0)
        gram_mat = jnp.dot(c_block, b_block.T, precision=highest)
        x_scaled = x_block * step_block[:, :, None]
        y_inner = jnp.einsum(
            "hij,jhp->ihp", decay_mat * gram_mat[None], x_scaled, precision=highest
        )
        y_state = jnp.exp(cum_decay)[:, :, None] * jnp.einsum(
            "in,hpn->ihp", c_block, state_now, precision=highest
        )
        tail_decay = jnp.exp(cum_decay[-1][None, :] - cum_decay)
        state_next = jnp.exp(cum_decay[-1])[:, None, None] * state_now + jnp.einsum(
            "jhp,jn->hpn", x_scaled * tail_decay[:, :, None], b_block, precision=highest
        )
        return (state_next, y_inner + y_state)

    start_state = jnp.zeros((head_count, head_size, state_size), jnp.float32)
    state_end, y_blocks = lax.scan(
        advance,
        start_state,
        (
            x_heads.reshape(blocks, block_len, head_count, head_size),
            b_rows.reshape(blocks, block_len, state_size),
            c_rows.reshape(blocks, block_len, state_size),
            step_size.reshape(blocks, block_len, head_count),
            log_decay.reshape(blocks, block_len, head_count),
        ),
    )
    return (y_blocks.reshape(length, head_count, head_size), state_end)


def chain_states(earlier, later):
    return (earlier[0] + later[0], jnp.exp(later[0])[:, None, None] * earlier[1] + later[1])


def row_slice(values, start_row, row_count):
    return lax.dynamic_slice_in_dim(values, start_row, row_count, 0)


def shards(
    input_raw,
    state_proj_raw,
    gate_branch,
    step_raw,
    convolution_taps,
    convolution_bias,
    step_bias,
    decay_log_rate,
    skip_weight,
    gated_norm_gain,
    output_weight,
    adapter_down,
    adapter_up,
    cotangent,
):
    highest = lax.Precision.HIGHEST
    tok_rows = input_raw.shape[1]
    inner_width = input_raw.shape[2]
    state_size = state_proj_raw.shape[2] // 2
    rim_width = convolution_taps.shape[0] - 1
    joined = jnp.concatenate([input_raw[0], state_proj_raw[0]], axis=1)
    before = passed_along(joined[tok_rows - rim_width :], ("context", "tensor"), 1)
    convolved = convolve(joined, before, convolution_taps, convolution_bias)
    x_heads_raw, z_heads, dt_heads = (
        lax.all_to_all(
            convolved[:, :inner_width], "tensor", split_axis=1, concat_axis=0, tiled=True
        ),
        lax.all_to_all(gate_branch[0], "tensor", split_axis=1, concat_axis=0, tiled=True),
        lax.all_to_all(step_raw[0], "tensor", split_axis=1, concat_axis=0, tiled=True),
    )
    shared = lax.all_gather(convolved[:, inner_width:], "tensor", axis=0, tiled=True)
    span_rows = x_heads_raw.shape[0]
    local_heads = dt_heads.shape[1]
    local_width = x_heads_raw.shape[1]
    head_size = local_width // local_heads
    x_heads = x_heads_raw.astype(jnp.float32).reshape(span_rows, local_heads, head_size)
    b_rows = shared[:, :state_size].astype(jnp.float32)
    c_rows = shared[:, state_size:].astype(jnp.float32)
    step_size = jax.nn.softplus(dt_heads.astype(jnp.float32) + step_bias[None, :])
    log_decay = -step_size * jnp.exp(decay_log_rate)[None, :]
    y_local, state_end = ssd_blocks(
        x_heads, b_rows, c_rows, step_size, log_decay, math.gcd(span_rows, 256)
    )
    log_total = jnp.sum(log_decay, axis=0)
    prior_total, incoming = entering(
        (log_total, state_end),
        "context",
        chain_states,
        (jnp.zeros_like(log_total), jnp.zeros_like(state_end)),
    )
    reach_decay = jnp.exp(jnp.cumsum(log_decay, axis=0))
    y_heads = y_local + reach_decay[:, :, None] * jnp.einsum(
        "tn,hpn->thp", c_rows, incoming, precision=highest
    )
    y_heads = y_heads + skip_weight[None, :, None] * x_heads
    gated = y_heads.reshape(span_rows, local_width) * jax.nn.silu(z_heads.astype(jnp.float32))
    squares = jnp.sum(gated * gated, axis=1)
    gated_output = (gated * gated_norm_gain[None, :]).astype(jnp.bfloat16)
    adapter_piece = jnp.dot(gated_output, adapter_down, preferred_element_type=jnp.float32)
    full_width = local_width * lax.axis_size("tensor")
    columns = lax.all_gather(output_weight, "fsdp", axis=1, tiled=True)
    own_start = lax.axis_index("tensor") * tok_rows
    sum_squares, adapter_all = (
        lax.psum(squares.astype(jnp.bfloat16), "tensor").astype(jnp.float32),
        lax.psum(adapter_piece.astype(jnp.bfloat16), "tensor").astype(jnp.float32),
    )
    scale_all = lax.rsqrt(sum_squares / full_width + epsilon)
    adapter_all = adapter_all.astype(jnp.bfloat16)
    leader = (lax.axis_index("tensor") == 0).astype(jnp.float32)
    start_row = jnp.int32(0)
    frozen_piece = jnp.dot(
        row_slice(gated_output, start_row, lax.axis_size("tensor") * tok_rows),
        columns,
        preferred_element_type=jnp.float32,
    )
    frozen_piece = frozen_piece + 2.0 * leader * jnp.dot(
        row_slice(adapter_all, start_row, lax.axis_size("tensor") * tok_rows),
        adapter_up,
        preferred_element_type=jnp.float32,
    )
    summed = lax.psum_scatter(
        (
            row_slice(scale_all, start_row, lax.axis_size("tensor") * tok_rows)[:, None]
            * frozen_piece
        ).astype(jnp.bfloat16),
        "tensor",
        scatter_dimension=0,
        tiled=True,
    )
    row_norm_scale = row_slice(scale_all, own_start, tok_rows)
    adapter_branch = row_slice(adapter_all, own_start, tok_rows)
    cotangent_rows = cotangent[0]
    token_total = (
        tok_rows * lax.axis_size("context") * lax.axis_size("tensor") * lax.axis_size("fsdp")
    )
    lowrank_factor = 2.0 / math.sqrt(token_total)
    weighted = lowrank_factor * row_norm_scale[:, None] * adapter_branch.astype(jnp.float32)
    grad_b_local = jnp.dot(weighted.T, cotangent_rows.astype(jnp.float32), precision=highest)
    adapter_gradient = (
        lowrank_factor
        * row_norm_scale[:, None]
        * jnp.dot(cotangent_rows, adapter_up.T, preferred_element_type=jnp.float32)
    )
    adapter_span = lax.all_gather(adapter_gradient, "tensor", axis=0, tiled=True)
    grad_a_local = jnp.dot(gated_output.astype(jnp.float32).T, adapter_span, precision=highest)
    grad_a, grad_b_part = lax.psum((grad_a_local, grad_b_local), ("context", "fsdp"))
    grad_b = lax.psum(grad_b_part.astype(jnp.bfloat16), "tensor").astype(jnp.float32)
    return (summed[None], grad_a, grad_b)


def solution(mesh):
    placed = (
        P("fsdp", ("context", "tensor"), None),
        P("fsdp", ("context", "tensor"), None),
        P("fsdp", ("context", "tensor"), None),
        P("fsdp", ("context", "tensor"), None),
        P(),
        P(),
        P("tensor"),
        P("tensor"),
        P("tensor"),
        P("tensor"),
        P("tensor", "fsdp"),
        P("tensor", None),
        P(),
        P("fsdp", ("context", "tensor"), None),
    )
    return jax.shard_map(
        shards,
        mesh=mesh,
        in_specs=placed,
        out_specs=(P("fsdp", ("context", "tensor"), None), P("tensor", None), P()),
        check_vma=False,
    )
```

profile of v0, /device:TPU:0, one launch (start us, length us, event | category | flops | bytes accessed | tf_op | source)
XLA Modules:
  0.0 443.3 jit_solution(7496762377417726398)
XLA Ops:
  8.3 4.9 %collective-permute-start = (bf16[3,5376]{1,0:T(4,128)(2,1)S(1)}, bf16[3,5376]{1,0:T(4,128)(2,1)S(1)}, u32[]{:S(2)}, u32[]{:S(2)}) collective-permute-start(bf16[3,5376]{1,0:T(4,128)(2,1)S(1)} %fusion.75), channel_id=1, source_target_pairs={{0,4},{4,8},{8,12},{12,16},{16,20},{20,24},{24,28},{1,5},{5,9},{9,... | collective-permute-start | bytes 96776 | tf_op jit(solution)/shard_map/ppermute | solution.py:13
  24.6 4.2 all-to-all-start.1
  30.3 19.2 %all_gather.21 = bf16[512,256]{1,0:T(8,128)(2,1)S(1)} all-gather(bf16[128,256]{1,0:T(8,128)(2,1)S(1)} %slice.84), channel_id=1, replica_groups=mesh['context'=2,'tensor'=4,'fsdp'=4] {'tensor'}, dimensions={0}, use_global_device_ids=true | all-gather | bytes 327680 | tf_op jit(solution)/shard_map/all_gather | solution.py:124
  51.1 5.4 %copy.68 = f32[4,128,1280]{1,0,2:T(4,128)S(1)} copy(f32[4,128,1280]{1,2,0:T(8,128)S(1)} %convert_bitcast_fusion.1) | data formatting | bytes 5242880 | tf_op jit(solution)/shard_map/convert_element_type | solution.py:129
  59.9 93.5 %while.4 = (s32[]{:T(128)}, f32[20,64,128]{2,1,0:T(8,128)}, f32[2,256,20,64]{1,0,3,2:T(2,128)}, f32[2,256,20]{1,0,2:T(2,128)}, f32[2,256,20,64]{1,0,3,2:T(2,128)...) while((s32[]{:T(128)}, f32[20,64,128]{2,1,0:T(8,128)}, ...), condition=%wide.region_3.4_spmd.clone.clone, body=%wide.region_0.3_spmd.clone.clone.sunk | while | flops 2122191872 | bytes 18280176 | solution.py:71
  66.2 6.0 %fusion.115 = f32[256,20,64]{0,2,1:T(8,128)S(1)} fusion(f32[256,256]{1,0:T(8,128)S(1)} %fusion.114, f32[20,256]{1,0:T(8,128)S(1)} %bitcast.176, pred[256,256]{1,0:T(8,128)(4,1)S(1)} %iota_compare_fusion.2, f32[1,256,20,64]{1,0,3,2:T(1,128)S(1)} %constant_dynamic-slice_fusion.5, f32[256,20]{0,1:T(8,128)S(1)} %bitcast.180), kind=kOutput, calls=%fused_computation.15.clone.1 | convolution fusion | flops 1012203520 | bytes 2990080 | tf_op jit(solution)/shard_map/while/body/eval_jaxpr/hij,jhp->ihp/dot_general | solution.py:58
  76.5 27.0 %dynamic_update_slice.7 = f32[2,256,20,64]{1,0,3,2:T(2,128)} dynamic-update-slice(f32[2,256,20,64]{1,0,3,2:T(2,128)} %get-tuple-element.267, f32[1,256,20,64]{1,0,3,2:T(1,128)S(1)} %copy.124, s32[]{:T(128)} %get-tuple-element.265, s32[]{:T(128)} %constant.41.clone.1..sunk, s32[]{:T(128)} %constant.41.clone.1..sunk, s32[]{:T(128)} %constant.41.clone.1..sunk) | dynamic-update-slice | bytes 2621444 | tf_op jit(solution)/shard_map/while/body/jit(dynamic_update_index_in_dim)/dynamic_update_slice | solution.py:71
  112.7 6.0 %fusion.115 = f32[256,20,64]{0,2,1:T(8,128)S(1)} fusion(f32[256,256]{1,0:T(8,128)S(1)} %fusion.114, f32[20,256]{1,0:T(8,128)S(1)} %bitcast.176, pred[256,256]{1,0:T(8,128)(4,1)S(1)} %iota_compare_fusion.2, f32[1,256,20,64]{1,0,3,2:T(1,128)S(1)} %constant_dynamic-slice_fusion.5, f32[256,20]{0,1:T(8,128)S(1)} %bitcast.180), kind=kOutput, calls=%fused_computation.15.clone.1 | convolution fusion | flops 1012203520 | bytes 2990080 | tf_op jit(solution)/shard_map/while/body/eval_jaxpr/hij,jhp->ihp/dot_general | solution.py:58
  123.3 27.0 %dynamic_update_slice.7 = f32[2,256,20,64]{1,0,3,2:T(2,128)} dynamic-update-slice(f32[2,256,20,64]{1,0,3,2:T(2,128)} %get-tuple-element.267, f32[1,256,20,64]{1,0,3,2:T(1,128)S(1)} %copy.124, s32[]{:T(128)} %get-tuple-element.265, s32[]{:T(128)} %constant.41.clone.1..sunk, s32[]{:T(128)} %constant.41.clone.1..sunk, s32[]{:T(128)} %constant.41.clone.1..sunk) | dynamic-update-slice | bytes 2621444 | tf_op jit(solution)/shard_map/while/body/jit(dynamic_update_index_in_dim)/dynamic_update_slice | solution.py:71
  156.2 3.5 all-to-all-start.2
  166.6 6.9 %all-to-all-done.2 = bf16[128,4,1280]{0,2,1:T(8,128)(2,1)S(1)} async-done(((bf16[128,4,1280]{0,2,1:T(8,128)(2,1)}), bf16[128,4,1280]{0,2,1:T(8,128)(2,1)S(1)}, u32[]{:S(2)}, u32[]{:S(2)}) %all-to-all-start.2) | async-done | bytes 1310752 | tf_op jit(solution)/shard_map/all_to_all | solution.py:121
  176.1 4.3 copy.79
  180.4 4.3 reshape.166
  186.8 4.9 %reshape.152 = f32[512,20,64]{0,2,1:T(8,128)} reshape(f32[2,256,20,64]{1,0,3,2:T(2,128)} %get-tuple-element.72) | data formatting | bytes 5242880 | tf_op jit(solution)/shard_map/reshape | solution.py:82
  191.8 6.3 %multiply_reduce_fusion = (bf16[512]{0:T(512)(128)(2,1)S(1)}, f32[512,20,64]{0,2,1:T(8,128)}) fusion(f32[512,20,64]{0,2,1:T(8,128)S(1)} %copy-done.6, f32[512,20,64]{0,2,1:T(8,128)} %reshape.165, f32[20]{0:T(128)S(1)} %copy-done.22, f32[512,20,64]{0,2,1:T(8,128)} %reshape.152, f32[40,64,128]{2,1,0:T(8,128)} %all-gather.7.cloned.1.call-done, ...), kind=kOutput, calls=%fused_computation.66 | convolution fusion | flops 1014169088 | bytes 11323393 | tf_op jit(solution)/shard_map/tn,hpn->thp/dot_general | solution.py:145
  198.1 3.4 copy.80
  204.7 15.3 %all-reduce.1 = (bf16[512,16]{0,1:T(8,128)(2,1)S(1)}, bf16[512]{0:T(512)(128)(2,1)S(1)}) all-reduce(bf16[512,16]{0,1:T(8,128)(2,1)S(1)} %convolution_convert_fusion, bf16[512]{0:T(512)(128)(2,1)S(1)} %get-tuple-element.195), channel_id=1, replica_groups=mesh['context'=2,'tensor'=4,'fsdp'=4] {'tensor'}, use_global_device_ids=true, to_apply=%region_9.10 | all-reduce | flops 8704 | bytes 34816 | tf_op jit(solution)/shard_map/psum | solution.py:158
  220.6 8.2 %all_gather.27 = f32[512,16]{0,1:T(8,128)S(1)} all-gather(f32[128,16]{0,1:T(8,128)S(1)} %convolution_multiply_fusion.1), channel_id=1, replica_groups=mesh['context'=2,'tensor'=4,'fsdp'=4] {'tensor'}, dimensions={0}, use_global_device_ids=true | all-gather | bytes 40960 | tf_op jit(solution)/shard_map/all_gather | solution.py:197
  228.8 51.7 %all-reduce.9 = bf16[16,2560]{1,0:T(8,128)(2,1)} all-reduce(f32[16,2560]{1,0:T(8,128)S(1)} %fusion.55), channel_id=1, replica_groups=mesh['context'=2,'tensor'=4,'fsdp'=4] {'context','fsdp'}, use_global_device_ids=true, to_apply=%region_12.13 | all-reduce | flops 40960 | bytes 245760 | tf_op jit(solution)/shard_map/psum | solution.py:199
  282.0 9.7 %all-gather.5.cloned.1.call-done = bf16[1280,2560]{1,0:T(8,128)(2,1)} async-done(((bf16[1280,640]{1,0:T(8,128)(2,1)}), bf16[1280,2560]{1,0:T(8,128)(2,1)}) %all-gather.5.cloned.1.call-update) | async-done | bytes 6553616 | tf_op jit(solution)/shard_map/all_gather | solution.py:154
  291.6 5.7 %fusion.84 = f32[512,2560]{1,0:T(8,128)S(1)} fusion(bf16[512,1280]{1,0:T(8,128)(2,1)S(1)} %fusion.52, bf16[1280,2560]{1,0:T(8,128)(2,1)} %all-gather.5.cloned.1.call-done), kind=kOutput, calls=%fused_computation.121 | convolution fusion | flops 3355443200 | bytes 13107200 | tf_op jit(solution)/shard_map/dot_general | solution.py:164
  299.8 35.1 %all-reduce.8.cloned.1.call-done = bf16[16,2560]{1,0:T(8,128)(2,1)} async-done(((bf16[16,2560]{1,0:T(8,128)(2,1)}), bf16[16,2560]{1,0:T(8,128)(2,1)}) %all-reduce.8.cloned.1.call-update) | async-done | bytes 81936 | tf_op jit(solution)/shard_map/psum | solution.py:200
  336.4 52.5 %all-reduce.6.cloned.1.call-done = f32[1280,16]{0,1:T(8,128)} async-done(((f32[1280,16]{0,1:T(8,128)}), f32[1280,16]{0,1:T(8,128)}) %all-reduce.6.cloned.1.call-update) | async-done | bytes 81936 | tf_op jit(solution)/shard_map/psum | solution.py:199
  388.9 46.4 %reduce-scatter.2.cloned.1.call-done = bf16[128,2560]{1,0:T(8,128)(2,1)} async-done(((bf16[512,2560]{1,0:T(8,128)(2,1)}), bf16[128,2560]{1,0:T(8,128)(2,1)}) %reduce-scatter.2.cloned.1.call-update) | async-done | bytes 655376 | tf_op jit(solution)/shard_map/reduce_scatter | solution.py:174
  (163 shorter events, 70.5 us)
Async XLA Ops:
  7.2 212.8 %copy-start = (bf16[1,128,2560]{2,1,0:T(8,128)(2,1)S(1)}, bf16[1,128,2560]{2,1,0:T(8,128)(2,1)}, u32[]{:S(2)}) copy-start(bf16[1,128,2560]{2,1,0:T(8,128)(2,1)} %param.29) | copy-start | bytes 1966084
  7.2 13.6 %copy-start.5 = (bf16[1,128,5120]{2,1,0:T(8,128)(2,1)S(1)}, bf16[1,128,5120]{2,1,0:T(8,128)(2,1)}, u32[]{:S(2)}) copy-start(bf16[1,128,5120]{2,1,0:T(8,128)(2,1)} %param.16) | copy-start | bytes 3932164
  7.2 13.6 %copy-start.11 = (bf16[1,128,256]{2,1,0:T(8,128)(2,1)S(1)}, bf16[1,128,256]{2,1,0:T(8,128)(2,1)}, u32[]{:S(2)}) copy-start(bf16[1,128,256]{2,1,0:T(8,128)(2,1)} %param.17) | copy-start | bytes 196612
  7.2 13.6 %copy-start.18 = (f32[5376]{0:T(1024)S(1)}, f32[5376]{0:T(1024)}, u32[]{:S(2)}) copy-start(f32[5376]{0:T(1024)} %param.21) | copy-start | bytes 64516
  8.3 10.8 %collective-permute-start = (bf16[3,5376]{1,0:T(4,128)(2,1)S(1)}, bf16[3,5376]{1,0:T(4,128)(2,1)S(1)}, u32[]{:S(2)}, u32[]{:S(2)}) collective-permute-start(bf16[3,5376]{1,0:T(4,128)(2,1)S(1)} %fusion.75), channel_id=1, source_target_pairs={{0,4},{4,8},{8,12},{12,16},{16,20},{20,24},{24,28},{1,5},{5,9},{9,... | collective-permute-start | bytes 96776 | tf_op jit(solution)/shard_map/ppermute | solution.py:13
  14.5 10.1 %all-to-all-start = ((bf16[128,4,20]{0,2,1:T(8,128)(2,1)}), bf16[128,4,20]{0,2,1:T(8,128)(2,1)S(1)}, u32[]{:S(2)}, u32[]{:S(2)}) async-start(bf16[128,4,20]{0,2,1:T(8,128)(2,1)} %all_to_all.30), calls=%async_computation | async-start | bytes 49152 | tf_op jit(solution)/shard_map/all_to_all | solution.py:122
  23.1 5.7 %copy-start.21 = (f32[20]{0:T(128)S(1)}, f32[20]{0:T(128)}, u32[]{:S(2)}) copy-start(f32[20]{0:T(128)} %param.23) | copy-start | bytes 244
  23.1 6.4 %copy-start.20 = (f32[20]{0:T(128)S(1)}, f32[20]{0:T(128)}, u32[]{:S(2)}) copy-start(f32[20]{0:T(128)} %param.22) | copy-start | bytes 244
  24.6 26.3 %all-to-all-start.1 = ((bf16[128,4,1280]{0,2,1:T(8,128)(2,1)}), bf16[128,4,1280]{0,2,1:T(8,128)(2,1)S(1)}, u32[]{:S(2)}, u32[]{:S(2)}) async-start(bf16[128,4,1280]{0,2,1:T(8,128)(2,1)} %bitcast.3), calls=%async_computation.1 | async-start | bytes 2621440 | tf_op jit(solution)/shard_map/all_to_all | solution.py:118
  28.7 163.0 %all-gather.7.cloned.1.call-start = ((), (), s32[]{:S(2)}) async-start(), calls=%async_computation.8 | async-start | bytes 1966080 | tf_op jit(solution)/shard_map/all_gather | solution.py:18
  63.0 9.1 %copy-start.7 = (f32[1,256,20]{1,2,0:T(8,128)}, f32[1,256,20]{1,2,0:T(8,128)S(1)}, u32[]{:S(2)}) copy-start(f32[1,256,20]{1,2,0:T(8,128)S(1)} %copy.123) | copy-start | bytes 61444 | tf_op jit(solution)/shard_map/while
  109.5 9.1 %copy-start.7 = (f32[1,256,20]{1,2,0:T(8,128)}, f32[1,256,20]{1,2,0:T(8,128)S(1)}, u32[]{:S(2)}) copy-start(f32[1,256,20]{1,2,0:T(8,128)S(1)} %copy.123) | copy-start | bytes 61444 | tf_op jit(solution)/shard_map/while
  153.5 138.1 %all-gather.5.cloned.1.call-start = ((), (), s32[]{:S(2)}) async-start(), calls=%async_computation.4 | async-start | bytes 8192000 | tf_op jit(solution)/shard_map/all_gather | solution.py:154
  154.8 5.1 %copy-start.23 = (u32[32]{0:T(128)S(1)}, u32[32]{0:T(128)}, u32[]{:S(2)}) copy-start(u32[32]{0:T(128)} %constant.76) | copy-start | bytes 388
  154.8 6.3 %copy-start.13 = (f32[4,128,20]{1,2,0:T(8,128)S(1)}, f32[4,128,20]{1,2,0:T(8,128)}, u32[]{:S(2)}) copy-start(f32[4,128,20]{1,2,0:T(8,128)} %copy-done.12) | copy-start | bytes 122884
  154.8 8.9 %copy-start.16 = (bf16[128,4,20]{0,2,1:T(8,128)(2,1)S(1)}, bf16[128,4,20]{0,2,1:T(8,128)(2,1)}, u32[]{:S(2)}) copy-start(bf16[128,4,20]{0,2,1:T(8,128)(2,1)} %copy-done.15) | copy-start | bytes 61444
  156.2 17.3 %all-to-all-start.2 = ((bf16[128,4,1280]{0,2,1:T(8,128)(2,1)}), bf16[128,4,1280]{0,2,1:T(8,128)(2,1)S(1)}, u32[]{:S(2)}, u32[]{:S(2)}) async-start(bf16[128,4,1280]{0,2,1:T(8,128)(2,1)} %bitcast.12), calls=%async_computation.2 | async-start | bytes 2621440 | tf_op jit(solution)/shard_map/all_to_all | solution.py:121
  159.8 175.1 %all-reduce.8.cloned.1.call-start = ((), (), s32[]{:S(2)}) async-start(), calls=%async_computation.7 | async-start | bytes 163840 | tf_op jit(solution)/shard_map/psum | solution.py:200
  186.8 4.9 %copy-start.6 = (f32[512,20,64]{0,2,1:T(8,128)S(1)}, f32[512,20,64]{0,2,1:T(8,128)}, u32[]{:S(2)}) copy-start(f32[512,20,64]{0,2,1:T(8,128)} %reshape.166) | copy-start | bytes 7864324
  186.8 4.9 %copy-start.10 = (bf16[512,256]{1,0:T(8,128)(2,1)S(1)}, bf16[512,256]{1,0:T(8,128)(2,1)}, u32[]{:S(2)}) copy-start(bf16[512,256]{1,0:T(8,128)(2,1)} %copy-done.9) | copy-start | bytes 786436
  186.8 4.9 %copy-start.22 = (f32[20]{0:T(128)S(1)}, f32[20]{0:T(128)}, u32[]{:S(2)}) copy-start(f32[20]{0:T(128)} %param.24) | copy-start | bytes 244
  201.5 18.9 %copy-start.14 = (bf16[16,2560]{1,0:T(8,128)(2,1)S(1)}, bf16[16,2560]{1,0:T(8,128)(2,1)}, u32[]{:S(2)}) copy-start(bf16[16,2560]{1,0:T(8,128)(2,1)} %param.28) | copy-start | bytes 245764
  280.6 108.3 %all-reduce.6.cloned.1.call-start = ((), (), s32[]{:S(2)}) async-start(), calls=%async_computation.6 | async-start | bytes 163840 | tf_op jit(solution)/shard_map/psum | solution.py:199
  281.9 153.3 %reduce-scatter.2.cloned.1.call-start = ((), (), s32[]{:S(2)}) async-start(), calls=%async_computation.5 | async-start | bytes 3276800 | tf_op jit(solution)/shard_map/reduce_scatter | solution.py:174
  (10 other events, 26.0 us)
Sparse Core Ops, SparseCore 0:
  153.6 9.6 all-gather.6
  164.9 126.6 all-gather.4
  295.1 39.6 all-reduce.7
  337.6 51.2 all-reduce.5
  392.3 42.9 reduce-scatter.1
where the time goes:
time: 448 us; the launch traced here: 443 us
  waiting for transfers between devices  151 us (34%)
  local copies, waits for them, and re-layouts  105 us (23%)
  blocking collectives  96.8 us (22%)
  matrix products  41.7 us (9%)
  other arithmetic  17.6 us (4%)
  starting transfers between devices  16 us (4%)
  between operations  14.8 us (3%)
    dynamic_update_slice x4, local copies, waits for them, and re-layouts, ssd_blocks(): lax.scan(advance, start_state, (x_heads.reshape(blocks, block_len, head_c...  56.8 us
    psum x1, waiting for transfers between devices, shards(): lax.psum((grad_a_local, grad_b_local), ('context', 'fsdp'))  52.5 us
    psum x1, blocking collectives, shards(): lax.psum((grad_a_local, grad_b_local), ('context', 'fsdp'))  51.7 us
    reduce_scatter x1, waiting for transfers between devices, shards(): lax.psum_scatter((row_slice(scale_all, start_row, lax.axis_size('tensor')...  46.4 us
    psum x1, waiting for transfers between devices, shards(): lax.psum(grad_b_part.astype(jnp.bfloat16), 'tensor').astype(jnp.float32)  35.1 us
    all_gather x1, blocking collectives, shards(): lax.all_gather(convolved[:, inner_width:], 'tensor', axis=0, tiled=True)  19.2 us
    psum x1, blocking collectives, shards(): lax.psum(adapter_piece.astype(jnp.bfloat16), 'tensor').astype(jnp.float32)  15.3 us
    dot_general x2, matrix products, advance(): jnp.einsum('hij,jhp->ihp', decay_mat * gram_mat[None], x_scaled, precisio...  11.9 us
  transfers between devices with their start and end apart: 9, of which 5 were waited for; matrix products, arithmetic and copies ran while one was open for 13% of the time, Pallas kernels for 0%

commit v1 on v0

--- a/solution.py
+++ b/solution.py
@@ -197,7 +197,9 @@
     adapter_span = lax.all_gather(adapter_gradient, "tensor", axis=0, tiled=True)
     grad_a_local = jnp.dot(gated_output.astype(jnp.float32).T, adapter_span, precision=highest)
     grad_a, grad_b_part = lax.psum((grad_a_local, grad_b_local), ("context", "fsdp"))
-    grad_b = lax.psum(grad_b_part.astype(jnp.bfloat16), "tensor").astype(jnp.float32)
+    grad_b = jnp.sum(lax.all_gather(grad_b_part.astype(jnp.bfloat16), "tensor"), axis=0).astype(
+        jnp.float32
+    )
     return (summed[None], grad_a, grad_b)
 
 

time: 448 us -> 397 us (0.89)
  waiting for transfers between devices: 151 us -> 114 us
  blocking collectives: 96.8 us -> 84.1 us
    psum x1, waiting for transfers between devices: 52.5 us -> 3.88 us  [shards(): lax.psum((grad_a_local, grad_b_local), ('context', 'fsdp'))]
    all_gather x1, waiting for transfers between devices: 9.67 us -> 55.9 us  [shards(): columns = lax.all_gather(output_weight, 'fsdp', axis=1, tiled=True)]
    psum x1 -> x0, waiting for transfers between devices: 35.1 us -> none  [shards(): lax.psum(grad_b_part.astype(jnp.bfloat16), 'tensor').astype(jnp.float32)]
    psum x1, blocking collectives: 51.7 us -> 28.9 us  [shards(): lax.psum((grad_a_local, grad_b_local), ('context', 'fsdp'))]
    all_gather x0 -> x1, blocking collectives: none -> 10.2 us  [shards(): lax.all_gather(grad_b_part.astype(jnp.bfloat16), 'tensor')]
  transfers between devices with their start and end apart: 9 -> 8, of which waited for: 5 -> 4; matrix products, arithmetic and copies ran while one was open for 13% -> 14% of each run, Pallas kernels for 0% -> 0%
where the time goes in v1:
time: 397 us; the launch traced here: 392 us
  waiting for transfers between devices  114 us (29%)
  local copies, waits for them, and re-layouts  105 us (26%)
  blocking collectives  84.1 us (21%)
  matrix products  41.7 us (11%)
  other arithmetic  16.7 us (4%)
  starting transfers between devices  16 us (4%)
  between operations  14.8 us (4%)
    dynamic_update_slice x4, local copies, waits for them, and re-layouts, ssd_blocks(): lax.scan(advance, start_state, (x_heads.reshape(blocks, block_len, head_c...  56.8 us
    all_gather x1, waiting for transfers between devices, shards(): columns = lax.all_gather(output_weight, 'fsdp', axis=1, tiled=True)  55.9 us
    reduce_scatter x1, waiting for transfers between devices, shards(): lax.psum_scatter((row_slice(scale_all, start_row, lax.axis_size('tensor')...  46.4 us
    psum x1, blocking collectives, shards(): lax.psum((grad_a_local, grad_b_local), ('context', 'fsdp'))  28.9 us
    all_gather x1, blocking collectives, shards(): lax.all_gather(convolved[:, inner_width:], 'tensor', axis=0, tiled=True)  19.2 us
    psum x1, blocking collectives, shards(): lax.psum(adapter_piece.astype(jnp.bfloat16), 'tensor').astype(jnp.float32)  15.3 us
    dot_general x2, matrix products, advance(): jnp.einsum('hij,jhp->ihp', decay_mat * gram_mat[None], x_scaled, precisio...  11.9 us
    convert_element_type x3, local copies, waits for them, and re-layouts, shards(): x_heads_raw.astype(jnp.float32).reshape(span_rows, local_heads, head_size)  10.9 us
  transfers between devices with their start and end apart: 8, of which 4 were waited for; matrix products, arithmetic and copies ran while one was open for 14% of the time, Pallas kernels for 0%

profile of v1, /device:TPU:0, one launch (start us, length us, event | category | flops | bytes accessed | tf_op | source)
XLA Modules:
  0.0 392.3 jit_solution(17924060496503463533)
XLA Ops:
  8.3 4.9 %collective-permute-start = (bf16[3,5376]{1,0:T(4,128)(2,1)S(1)}, bf16[3,5376]{1,0:T(4,128)(2,1)S(1)}, u32[]{:S(2)}, u32[]{:S(2)}) collective-permute-start(bf16[3,5376]{1,0:T(4,128)(2,1)S(1)} %fusion.75), channel_id=1, source_target_pairs={{0,4},{4,8},{8,12},{12,16},{16,20},{20,24},{24,28},{1,5},{5,9},{9,... | collective-permute-start | bytes 96776 | tf_op jit(solution)/shard_map/ppermute | solution.py:13
  24.6 4.2 %all-to-all-start.1 = ((bf16[128,4,1280]{0,2,1:T(8,128)(2,1)}), bf16[128,4,1280]{0,2,1:T(8,128)(2,1)S(1)}, u32[]{:S(2)}, u32[]{:S(2)}) async-start(bf16[128,4,1280]{0,2,1:T(8,128)(2,1)} %bitcast.3), calls=%async_computation.1 | async-start | bytes 2621440 | tf_op jit(solution)/shard_map/all_to_all | solution.py:118
  30.3 19.2 %all_gather.27 = bf16[512,256]{1,0:T(8,128)(2,1)S(1)} all-gather(bf16[128,256]{1,0:T(8,128)(2,1)S(1)} %slice.84), channel_id=1, replica_groups=mesh['context'=2,'tensor'=4,'fsdp'=4] {'tensor'}, dimensions={0}, use_global_device_ids=true | all-gather | bytes 327680 | tf_op jit(solution)/shard_map/all_gather | solution.py:124
  51.1 5.4 %copy.68 = f32[4,128,1280]{1,0,2:T(4,128)S(1)} copy(f32[4,128,1280]{1,2,0:T(8,128)S(1)} %convert_bitcast_fusion.1) | data formatting | bytes 5242880 | tf_op jit(solution)/shard_map/convert_element_type | solution.py:129
  59.9 93.5 %while.4 = (s32[]{:T(128)}, f32[20,64,128]{2,1,0:T(8,128)}, f32[2,256,20,64]{1,0,3,2:T(2,128)}, f32[2,256,20]{1,0,2:T(2,128)}, f32[2,256,20,64]{1,0,3,2:T(2,128)...) while((s32[]{:T(128)}, f32[20,64,128]{2,1,0:T(8,128)}, ...), condition=%wide.region_3.4_spmd.clone.clone, body=%wide.region_0.3_spmd.clone.clone.sunk | while | flops 2122191872 | bytes 18280176 | solution.py:71
  66.2 6.0 %fusion.115 = f32[256,20,64]{0,2,1:T(8,128)S(1)} fusion(f32[256,256]{1,0:T(8,128)S(1)} %fusion.114, f32[20,256]{1,0:T(8,128)S(1)} %bitcast.177, pred[256,256]{1,0:T(8,128)(4,1)S(1)} %iota_compare_fusion.2, f32[1,256,20,64]{1,0,3,2:T(1,128)S(1)} %constant_dynamic-slice_fusion.5, f32[256,20]{0,1:T(8,128)S(1)} %bitcast.181), kind=kOutput, calls=%fused_computation.15.clone.1 | convolution fusion | flops 1012203520 | bytes 2990080 | tf_op jit(solution)/shard_map/while/body/eval_jaxpr/hij,jhp->ihp/dot_general | solution.py:58
  76.5 27.0 %dynamic_update_slice.7 = f32[2,256,20,64]{1,0,3,2:T(2,128)} dynamic-update-slice(f32[2,256,20,64]{1,0,3,2:T(2,128)} %get-tuple-element.267, f32[1,256,20,64]{1,0,3,2:T(1,128)S(1)} %copy.124, s32[]{:T(128)} %get-tuple-element.265, s32[]{:T(128)} %constant.43.clone.1..sunk, s32[]{:T(128)} %constant.43.clone.1..sunk, s32[]{:T(128)} %constant.43.clone.1..sunk) | dynamic-update-slice | bytes 2621444 | tf_op jit(solution)/shard_map/while/body/jit(dynamic_update_index_in_dim)/dynamic_update_slice | solution.py:71
  112.7 6.0 %fusion.115 = f32[256,20,64]{0,2,1:T(8,128)S(1)} fusion(f32[256,256]{1,0:T(8,128)S(1)} %fusion.114, f32[20,256]{1,0:T(8,128)S(1)} %bitcast.177, pred[256,256]{1,0:T(8,128)(4,1)S(1)} %iota_compare_fusion.2, f32[1,256,20,64]{1,0,3,2:T(1,128)S(1)} %constant_dynamic-slice_fusion.5, f32[256,20]{0,1:T(8,128)S(1)} %bitcast.181), kind=kOutput, calls=%fused_computation.15.clone.1 | convolution fusion | flops 1012203520 | bytes 2990080 | tf_op jit(solution)/shard_map/while/body/eval_jaxpr/hij,jhp->ihp/dot_general | solution.py:58
  123.3 27.0 %dynamic_update_slice.7 = f32[2,256,20,64]{1,0,3,2:T(2,128)} dynamic-update-slice(f32[2,256,20,64]{1,0,3,2:T(2,128)} %get-tuple-element.267, f32[1,256,20,64]{1,0,3,2:T(1,128)S(1)} %copy.124, s32[]{:T(128)} %get-tuple-element.265, s32[]{:T(128)} %constant.43.clone.1..sunk, s32[]{:T(128)} %constant.43.clone.1..sunk, s32[]{:T(128)} %constant.43.clone.1..sunk) | dynamic-update-slice | bytes 2621444 | tf_op jit(solution)/shard_map/while/body/jit(dynamic_update_index_in_dim)/dynamic_update_slice | solution.py:71
  156.2 3.5 all-to-all-start.2
  166.6 6.9 %all-to-all-done.2 = bf16[128,4,1280]{0,2,1:T(8,128)(2,1)S(1)} async-done(((bf16[128,4,1280]{0,2,1:T(8,128)(2,1)}), bf16[128,4,1280]{0,2,1:T(8,128)(2,1)S(1)}, u32[]{:S(2)}, u32[]{:S(2)}) %all-to-all-start.2) | async-done | bytes 1310752 | tf_op jit(solution)/shard_map/all_to_all | solution.py:121
  176.1 4.3 %copy.79 = f32[4,128,1280]{1,0,2:T(4,128)} copy(f32[4,128,1280]{2,1,0:T(8,128)} %convert_bitcast_fusion) | data formatting | bytes 5242880 | tf_op jit(solution)/shard_map/convert_element_type | solution.py:149
  180.4 4.3 %reshape.166 = f32[512,20,64]{0,2,1:T(8,128)} reshape(f32[4,128,1280]{1,0,2:T(4,128)} %copy.79) | data formatting | bytes 5242880 | tf_op jit(solution)/shard_map/convert_element_type | solution.py:149
  186.8 4.9 %reshape.152 = f32[512,20,64]{0,2,1:T(8,128)} reshape(f32[2,256,20,64]{1,0,3,2:T(2,128)} %get-tuple-element.72) | data formatting | bytes 5242880 | tf_op jit(solution)/shard_map/reshape | solution.py:82
  191.8 6.3 %multiply_reduce_fusion = (bf16[512]{0:T(512)(128)(2,1)S(1)}, f32[512,20,64]{0,2,1:T(8,128)}) fusion(f32[512,20,64]{0,2,1:T(8,128)S(1)} %copy-done.6, f32[512,20,64]{0,2,1:T(8,128)} %reshape.165, f32[20]{0:T(128)S(1)} %copy-done.22, f32[512,20,64]{0,2,1:T(8,128)} %reshape.152, f32[40,64,128]{2,1,0:T(8,128)} %all-gather.8.cloned.1.call-done, ...), kind=kOutput, calls=%fused_computation.66 | convolution fusion | flops 1014169088 | bytes 11323393 | tf_op jit(solution)/shard_map/tn,hpn->thp/dot_general | solution.py:145
  198.1 3.4 copy.80
  204.7 15.3 %all-reduce.1 = (bf16[512,16]{0,1:T(8,128)(2,1)S(1)}, bf16[512]{0:T(512)(128)(2,1)S(1)}) all-reduce(bf16[512,16]{0,1:T(8,128)(2,1)S(1)} %convolution_convert_fusion, bf16[512]{0:T(512)(128)(2,1)S(1)} %get-tuple-element.195), channel_id=1, replica_groups=mesh['context'=2,'tensor'=4,'fsdp'=4] {'tensor'}, use_global_device_ids=true, to_apply=%region_9.10 | all-reduce | flops 8704 | bytes 34816 | tf_op jit(solution)/shard_map/psum | solution.py:158
  220.3 8.2 %all_gather.33 = f32[512,16]{0,1:T(8,128)S(1)} all-gather(f32[128,16]{0,1:T(8,128)S(1)} %convolution_multiply_fusion.1), channel_id=1, replica_groups=mesh['context'=2,'tensor'=4,'fsdp'=4] {'tensor'}, dimensions={0}, use_global_device_ids=true | all-gather | bytes 40960 | tf_op jit(solution)/shard_map/all_gather | solution.py:197
  229.8 55.9 %all-gather.6.cloned.1.call-done = bf16[1280,2560]{1,0:T(8,128)(2,1)} async-done(((bf16[1280,640]{1,0:T(8,128)(2,1)}), bf16[1280,2560]{1,0:T(8,128)(2,1)}) %all-gather.6.cloned.1.call-update) | async-done | bytes 6553616 | tf_op jit(solution)/shard_map/all_gather | solution.py:154
  285.7 5.7 %fusion.84 = f32[512,2560]{1,0:T(8,128)S(1)} fusion(bf16[512,1280]{1,0:T(8,128)(2,1)S(1)} %fusion.52, bf16[1280,2560]{1,0:T(8,128)(2,1)} %all-gather.6.cloned.1.call-done), kind=kOutput, calls=%fused_computation.121 | convolution fusion | flops 3355443200 | bytes 13107200 | tf_op jit(solution)/shard_map/dot_general | solution.py:164
  294.2 28.9 %all-reduce.6 = bf16[16,2560]{1,0:T(8,128)(2,1)S(1)} all-reduce(f32[16,2560]{1,0:T(8,128)S(1)} %fusion.55), channel_id=1, replica_groups=mesh['context'=2,'tensor'=4,'fsdp'=4] {'context','fsdp'}, use_global_device_ids=true, to_apply=%region_12.13 | all-reduce | flops 40960 | bytes 245760 | tf_op jit(solution)/shard_map/psum | solution.py:199
  323.1 10.2 %all-gather.2 = bf16[64,2560]{1,0:T(8,128)(2,1)S(1)} all-gather(bf16[16,2560]{1,0:T(8,128)(2,1)S(1)} %all-reduce.6), channel_id=4, replica_groups=mesh['context'=2,'tensor'=4,'fsdp'=4] {'tensor'}, dimensions={0}, use_global_device_ids=true | all-gather | bytes 409600 | tf_op jit(solution)/shard_map/all_gather | solution.py:200
  334.0 3.9 all-reduce.5.cloned.1.call-done
  337.9 46.4 %reduce-scatter.2.cloned.1.call-done = bf16[128,2560]{1,0:T(8,128)(2,1)} async-done(((bf16[512,2560]{1,0:T(8,128)(2,1)}), bf16[128,2560]{1,0:T(8,128)(2,1)}) %reduce-scatter.2.cloned.1.call-update) | async-done | bytes 655376 | tf_op jit(solution)/shard_map/reduce_scatter | solution.py:174
  (162 shorter events, 69.6 us)
Async XLA Ops:
  7.2 212.8 %copy-start = (bf16[1,128,2560]{2,1,0:T(8,128)(2,1)S(1)}, bf16[1,128,2560]{2,1,0:T(8,128)(2,1)}, u32[]{:S(2)}) copy-start(bf16[1,128,2560]{2,1,0:T(8,128)(2,1)} %param.29) | copy-start | bytes 1966084
  7.2 13.6 %copy-start.5 = (bf16[1,128,5120]{2,1,0:T(8,128)(2,1)S(1)}, bf16[1,128,5120]{2,1,0:T(8,128)(2,1)}, u32[]{:S(2)}) copy-start(bf16[1,128,5120]{2,1,0:T(8,128)(2,1)} %param.16) | copy-start | bytes 3932164
  7.2 13.6 %copy-start.11 = (bf16[1,128,256]{2,1,0:T(8,128)(2,1)S(1)}, bf16[1,128,256]{2,1,0:T(8,128)(2,1)}, u32[]{:S(2)}) copy-start(bf16[1,128,256]{2,1,0:T(8,128)(2,1)} %param.17) | copy-start | bytes 196612
  7.2 13.6 %copy-start.18 = (f32[5376]{0:T(1024)S(1)}, f32[5376]{0:T(1024)}, u32[]{:S(2)}) copy-start(f32[5376]{0:T(1024)} %param.21) | copy-start | bytes 64516
  8.3 10.8 %collective-permute-start = (bf16[3,5376]{1,0:T(4,128)(2,1)S(1)}, bf16[3,5376]{1,0:T(4,128)(2,1)S(1)}, u32[]{:S(2)}, u32[]{:S(2)}) collective-permute-start(bf16[3,5376]{1,0:T(4,128)(2,1)S(1)} %fusion.75), channel_id=1, source_target_pairs={{0,4},{4,8},{8,12},{12,16},{16,20},{20,24},{24,28},{1,5},{5,9},{9,... | collective-permute-start | bytes 96776 | tf_op jit(solution)/shard_map/ppermute | solution.py:13
  14.5 10.1 %all-to-all-start = ((bf16[128,4,20]{0,2,1:T(8,128)(2,1)}), bf16[128,4,20]{0,2,1:T(8,128)(2,1)S(1)}, u32[]{:S(2)}, u32[]{:S(2)}) async-start(bf16[128,4,20]{0,2,1:T(8,128)(2,1)} %all_to_all.30), calls=%async_computation | async-start | bytes 49152 | tf_op jit(solution)/shard_map/all_to_all | solution.py:122
  23.1 5.7 %copy-start.21 = (f32[20]{0:T(128)S(1)}, f32[20]{0:T(128)}, u32[]{:S(2)}) copy-start(f32[20]{0:T(128)} %param.23) | copy-start | bytes 244
  23.1 6.4 %copy-start.20 = (f32[20]{0:T(128)S(1)}, f32[20]{0:T(128)}, u32[]{:S(2)}) copy-start(f32[20]{0:T(128)} %param.22) | copy-start | bytes 244
  24.6 26.3 %all-to-all-start.1 = ((bf16[128,4,1280]{0,2,1:T(8,128)(2,1)}), bf16[128,4,1280]{0,2,1:T(8,128)(2,1)S(1)}, u32[]{:S(2)}, u32[]{:S(2)}) async-start(bf16[128,4,1280]{0,2,1:T(8,128)(2,1)} %bitcast.3), calls=%async_computation.1 | async-start | bytes 2621440 | tf_op jit(solution)/shard_map/all_to_all | solution.py:118
  28.7 163.0 %all-gather.8.cloned.1.call-start = ((), (), s32[]{:S(2)}) async-start(), calls=%async_computation.7 | async-start | bytes 1966080 | tf_op jit(solution)/shard_map/all_gather | solution.py:18
  63.0 9.1 %copy-start.7 = (f32[1,256,20]{1,2,0:T(8,128)}, f32[1,256,20]{1,2,0:T(8,128)S(1)}, u32[]{:S(2)}) copy-start(f32[1,256,20]{1,2,0:T(8,128)S(1)} %copy.123) | copy-start | bytes 61444 | tf_op jit(solution)/shard_map/while
  109.5 9.1 %copy-start.7 = (f32[1,256,20]{1,2,0:T(8,128)}, f32[1,256,20]{1,2,0:T(8,128)S(1)}, u32[]{:S(2)}) copy-start(f32[1,256,20]{1,2,0:T(8,128)S(1)} %copy.123) | copy-start | bytes 61444 | tf_op jit(solution)/shard_map/while
  153.5 132.2 %all-gather.6.cloned.1.call-start = ((), (), s32[]{:S(2)}) async-start(), calls=%async_computation.4 | async-start | bytes 8192000 | tf_op jit(solution)/shard_map/all_gather | solution.py:154
  154.8 5.1 %copy-start.23 = (u32[32]{0:T(128)S(1)}, u32[32]{0:T(128)}, u32[]{:S(2)}) copy-start(u32[32]{0:T(128)} %constant.78) | copy-start | bytes 388
  154.8 6.3 %copy-start.13 = (f32[4,128,20]{1,2,0:T(8,128)S(1)}, f32[4,128,20]{1,2,0:T(8,128)}, u32[]{:S(2)}) copy-start(f32[4,128,20]{1,2,0:T(8,128)} %copy-done.12) | copy-start | bytes 122884
  154.8 8.9 %copy-start.16 = (bf16[128,4,20]{0,2,1:T(8,128)(2,1)S(1)}, bf16[128,4,20]{0,2,1:T(8,128)(2,1)}, u32[]{:S(2)}) copy-start(bf16[128,4,20]{0,2,1:T(8,128)(2,1)} %copy-done.15) | copy-start | bytes 61444
  156.2 17.3 %all-to-all-start.2 = ((bf16[128,4,1280]{0,2,1:T(8,128)(2,1)}), bf16[128,4,1280]{0,2,1:T(8,128)(2,1)S(1)}, u32[]{:S(2)}, u32[]{:S(2)}) async-start(bf16[128,4,1280]{0,2,1:T(8,128)(2,1)} %bitcast.12), calls=%async_computation.2 | async-start | bytes 2621440 | tf_op jit(solution)/shard_map/all_to_all | solution.py:121
  159.8 178.1 %all-reduce.5.cloned.1.call-start = ((), (), s32[]{:S(2)}) async-start(), calls=%async_computation.6 | async-start | bytes 163840 | tf_op jit(solution)/shard_map/psum | solution.py:199
  180.4 4.3 %copy-start.2 = (f32[4,128,1280]{1,0,2:T(4,128)S(1)}, f32[4,128,1280]{1,0,2:T(4,128)}, u32[]{:S(2)}) copy-start(f32[4,128,1280]{1,0,2:T(4,128)} %copy-done.1) | copy-start | bytes 7864324
  186.8 4.9 %copy-start.6 = (f32[512,20,64]{0,2,1:T(8,128)S(1)}, f32[512,20,64]{0,2,1:T(8,128)}, u32[]{:S(2)}) copy-start(f32[512,20,64]{0,2,1:T(8,128)} %reshape.166) | copy-start | bytes 7864324
  186.8 4.9 %copy-start.10 = (bf16[512,256]{1,0:T(8,128)(2,1)S(1)}, bf16[512,256]{1,0:T(8,128)(2,1)}, u32[]{:S(2)}) copy-start(bf16[512,256]{1,0:T(8,128)(2,1)} %copy-done.9) | copy-start | bytes 786436
  186.8 4.9 %copy-start.22 = (f32[20]{0:T(128)S(1)}, f32[20]{0:T(128)}, u32[]{:S(2)}) copy-start(f32[20]{0:T(128)} %param.24) | copy-start | bytes 244
  201.5 18.5 %copy-start.14 = (bf16[16,2560]{1,0:T(8,128)(2,1)S(1)}, bf16[16,2560]{1,0:T(8,128)(2,1)}, u32[]{:S(2)}) copy-start(bf16[16,2560]{1,0:T(8,128)(2,1)} %param.28) | copy-start | bytes 245764
  229.7 154.6 %reduce-scatter.2.cloned.1.call-start = ((), (), s32[]{:S(2)}) async-start(), calls=%async_computation.5 | async-start | bytes 3276800 | tf_op jit(solution)/shard_map/reduce_scatter | solution.py:174
  (9 other events, 21.8 us)
Sparse Core Ops, SparseCore 0:
  153.6 9.6 all-gather.7
  164.9 120.7 all-gather.5
  288.6 49.2 all-reduce.4
  341.3 42.9 reduce-scatter.1
